TPU v7x, 32 devices: a whole 2x2x4 slice. The times are simulated.
32 devices in a mesh: grid: 8 (over y, x, core), rows: 4 (over z).
Axes of the slice: x: 2, y: 2, z: 4, core: 2. Of those that a mesh axis runs over, the one named last changes fastest.
Arguments:
- density: bfloat16 [32, 128, 4096], P(None, 'rows', 'grid'), as said below
- basis_values: bfloat16 [16, 16, 128, 512], P('grid', None, 'rows'), may hold values from -0.59765625 to 0.59765625
- grid_points: float32 [16, 3, 512], P('grid'), may hold values from -4 to 4
- grid_weights: float32 [16, 512], P('grid'), may hold values from 0.05 to 1
- screened_blocks: int32 [16, 16], P('grid'), may hold values from 0 to 31, as said below
Outputs:
- exchange: float32 [32, 128, 4096], P(None, 'rows', 'grid')
Inputs may be any that keep to these rules, and one draw needn't show every extreme that they name: density is symmetric: density[a, i, b * 128 + j] equals density[b, j, a * 128 + i]. `screened_blocks`: each row holds 16 distinct block numbers.
All inputs are finite; a program needn't handle non-finite values.
Results may differ from a plain program's by a relative error of at most 0.00055.
The roundings to bfloat16 on the way count: a program that leaves them out, or rounds other values in their place, can miss the bound.
Values may be sent and summed in bfloat16 or wider, within the bound.
A program may use at most 128 MiB of HBM per device.

v0:
```python
import jax
import jax.numpy as jnp
from jax import lax
from jax.sharding import PartitionSpec as P


def body(density, basis_values, grid_points, grid_weights, screened_blocks):
    nblocks = density.shape[0]
    rows_mine = density.shape[1]
    block_size = rows_mine * lax.axis_size("rows")
    nbasis = nblocks * block_size
    nsig = basis_values.shape[1]
    npoints = basis_values.shape[3]
    stripe = lax.all_gather(density, "grid", axis=2, tiled=True)
    totals = jnp.zeros((nblocks, rows_mine, nblocks, block_size), jnp.float32)
    for batch_index in range(basis_values.shape[0]):
        blocks = screened_blocks[batch_index]
        row_pick = jnp.take(stripe, blocks, axis=0).reshape(nsig * rows_mine, nblocks, block_size)
        chosen = jnp.take(row_pick, blocks, axis=1)
        local_values = basis_values[batch_index]
        x_mine = local_values.reshape(nsig * rows_mine, npoints)
        fsum = jnp.einsum(
            "mtk,tkp->mp",
            chosen,
            lax.all_gather(local_values, "rows", axis=1, tiled=True),
            preferred_element_type=jnp.float32,
        )
        fmat = fsum.astype(jnp.bfloat16)
        intersection_part = lax.dot_general(
            x_mine, fmat, (((0,), (0,)), ((), ())), preferred_element_type=jnp.float32
        )
        intersection = lax.psum(intersection_part, "rows")
        places = grid_points[batch_index]
        weights = grid_weights[batch_index]
        diffs = places[:, :, None] - places[:, None, :]
        kern = 1.0 / jnp.sqrt(jnp.sum(diffs * diffs, axis=0) + 0.5)
        mixed = (weights[:, None] * kern * intersection).astype(jnp.bfloat16)
        potential = (
            jnp.dot(x_mine, mixed, preferred_element_type=jnp.float32) * weights[None, :]
        ).astype(jnp.bfloat16)
        potential = potential.reshape(nsig, rows_mine, npoints)
        block_k = jnp.einsum(
            "mp,tkp->mtk",
            x_mine,
            lax.all_gather(potential, "rows", axis=1, tiled=True),
            preferred_element_type=jnp.float32,
        )
        block_k = block_k.reshape(nsig, rows_mine, nsig, block_size)
        totals = totals.at[blocks[:, None], :, blocks[None, :], :].add(
            block_k.transpose(0, 2, 1, 3)
        )
    return lax.psum_scatter(
        totals.reshape(nblocks, rows_mine, nbasis), "grid", scatter_dimension=2, tiled=True
    )


def solution(mesh):
    placed = (
        P(None, "rows", "grid"),
        P("grid", None, "rows", None),
        P("grid", None, None),
        P("grid", None),
        P("grid", None),
    )
    return jax.shard_map(
        body, mesh=mesh, in_specs=placed, out_specs=P(None, "rows", "grid"), check_vma=False
    )
```

profile of v0, /device:TPU:0, one launch (start us, length us, event | category | flops | bytes accessed | tf_op | source)
XLA Modules:
  0.0 572.5 jit_solution(16403228100501752769)
XLA Ops:
  7.3 2.3 fusion.56
  10.5 57.3 %all-gather.8.cloned.1.call-done = bf16[32,32,4096]{2,1,0:T(8,128)(2,1)} async-done(((bf16[32,32,512]{2,1,0:T(8,128)(2,1)}), bf16[32,32,4096]{2,1,0:T(8,128)(2,1)}) %all-gather.8.cloned.1.call-update) | async-done | bytes 8388624 | tf_op jit(solution)/shard_map/all_gather | solution.py:14
  67.8 6.2 %gather_fusion.2 = bf16[16,32,4096]{2,1,0:T(8,128)(2,1)} fusion(bf16[32,32,4096]{2,1,0:T(8,128)(2,1)} %all-gather.8.cloned.1.call-done, s32[1024]{0:T(1024)S(1)} %pad_clamp_fusion), kind=kCustom, calls=%fused_computation.2.clone | custom fusion | bytes 8388672 | tf_op jit(solution)/shard_map/jit(_take)/gather | solution.py:18
  74.0 2.7 broadcast_select_fusion
  76.7 1.3 copy.31
  78.0 3.6 copy.23
  81.6 3.1 gather_fusion.3
  84.8 6.2 %gather_fusion = bf16[16,32,4096]{2,1,0:T(8,128)(2,1)} fusion(bf16[32,32,4096]{2,1,0:T(8,128)(2,1)} %all-gather.8.cloned.1.call-done, s32[1024]{0:T(1024)S(1)} %pad_clamp_fusion.1), kind=kCustom, calls=%fused_computation.clone | custom fusion | bytes 8388672 | tf_op jit(solution)/shard_map/jit(_take)/gather | solution.py:18
  91.0 2.7 broadcast_select_fusion.1
  93.6 1.3 copy.30
  94.9 3.6 copy.19
  98.5 4.4 gather_fusion.1
  102.9 12.2 %all-gather.16.cloned.1.call-done = bf16[1,16,128,512]{3,2,1,0:T(8,128)(2,1)} async-done(((bf16[1,16,32,512]{3,2,1,0:T(8,128)(2,1)}), bf16[1,16,128,512]{3,2,1,0:T(8,128)(2,1)}) %all-gather.16.cloned.1.call-update) | async-done | bytes 2097168 | tf_op jit(solution)/shard_map/all_gather | solution.py:25
  115.1 4.3 convolution_bitcast_fusion.2
  119.4 41.8 %all-gather.14.cloned.1.call-done = bf16[1,16,128,512]{3,2,1,0:T(8,128)(2,1)} async-done(((bf16[1,16,32,512]{3,2,1,0:T(8,128)(2,1)}), bf16[1,16,128,512]{3,2,1,0:T(8,128)(2,1)}) %all-gather.14.cloned.1.call-update) | async-done | bytes 2097168 | tf_op jit(solution)/shard_map/all_gather | solution.py:25
  161.2 4.9 convolution_bitcast_fusion.3
  166.9 84.3 %all-reduce.3.cloned.1.call-done = (f32[512,512]{0,1:T(8,128)}, f32[512,512]{0,1:T(8,128)}) async-done(((f32[512,512]{0,1:T(8,128)}, f32[512,512]{0,1:T(8,128)}), (f32[512,512]{0,1:T(8,128)}, f32[512,512]{0,1:T(8,128)})) %all-reduce.3.cloned.1.call-update) | async-done | bytes 2097168 | tf_op jit(solution)/shard_map/psum | solution.py:32
  251.2 2.5 fusion.20
  254.5 2.5 fusion.21
  257.6 41.0 %all-gather.10.cloned.1.call-done = bf16[16,128,512]{2,1,0:T(8,128)(2,1)} async-done(((bf16[16,32,512]{2,1,0:T(8,128)(2,1)}), bf16[16,128,512]{2,1,0:T(8,128)(2,1)}) %all-gather.10.cloned.1.call-update) | async-done | bytes 2097168 | tf_op jit(solution)/shard_map/all_gather | solution.py:45
  298.6 4.8 convolution_bitcast_fusion.1
  303.4 5.5 copy.20
  309.0 5.5 copy.21
  314.4 30.1 %all-gather.12.cloned.1.call-done = bf16[16,128,512]{2,1,0:T(8,128)(2,1)} async-done(((bf16[16,32,512]{2,1,0:T(8,128)(2,1)}), bf16[16,128,512]{2,1,0:T(8,128)(2,1)}) %all-gather.12.cloned.1.call-update) | async-done | bytes 2097168 | tf_op jit(solution)/shard_map/all_gather | solution.py:45
  344.5 4.8 convolution_bitcast_fusion
  349.3 5.5 copy.24
  354.8 5.5 copy.25
  360.3 7.9 %broadcast_in_dim.45 = f32[32,32,32,128]{3,1,2,0:T(8,128)} broadcast(f32[]{:T(128)} %constant.20.clone.1), dimensions={} | broadcast | bytes 16777220 | tf_op jit(solution)/shard_map/broadcast_in_dim | solution.py:15
  368.2 35.3 %scatter_fusion = f32[32,32,32,128]{3,1,2,0:T(8,128)} fusion(f32[32,32,32,128]{3,1,2,0:T(8,128)} %broadcast_in_dim.45, s32[256]{0:T(256)S(1)} %reshape.132, f32[256,32,128]{2,1,0:T(8,128)} %bitcast.123), kind=kCustom, calls=%fused_computation.4 | custom fusion | flops 1048576 | bytes 12584960 | tf_op jit(solution)/shard_map/scatter-add | solution.py:49
  403.5 35.3 %scatter_fusion.1 = f32[32,32,32,128]{3,1,2,0:T(8,128)} fusion(f32[32,32,32,128]{3,1,2,0:T(8,128)} %scatter_fusion, s32[256]{0:T(256)S(1)} %reshape.138, f32[256,32,128]{2,1,0:T(8,128)} %bitcast.124), kind=kCustom, calls=%fused_computation.5 | custom fusion | flops 1048576 | bytes 12584960 | tf_op jit(solution)/shard_map/scatter-add | solution.py:49
  438.9 11.7 %copy_bitcast_fusion = f32[32,32,4096]{2,1,0:T(8,128)} fusion(f32[32,32,32,128]{3,1,2,0:T(8,128)} %scatter_fusion.1), kind=kLoop, calls=%fused_computation.6 | loop fusion | bytes 33554432 | tf_op jit(solution)/shard_map/reshape | solution.py:53
  450.6 115.0 %reduce-scatter.2.cloned.1.call-done = f32[32,32,512]{2,1,0:T(8,128)} async-done(((f32[32,32,4096]{2,1,0:T(8,128)}), f32[32,32,512]{2,1,0:T(8,128)}) %reduce-scatter.2.cloned.1.call-update) | async-done | bytes 2097168 | tf_op jit(solution)/shard_map/reduce_scatter | solution.py:52
  (42 shorter events, 3.6 us)
Async XLA Ops:
  6.5 3.9 copy-start.4
  6.5 61.3 %all-gather.8.cloned.1.call-start = ((), (), s32[]{:S(2)}) async-start(), calls=%async_computation.1 | async-start | bytes 9437184 | tf_op jit(solution)/shard_map/all_gather | solution.py:14
  7.3 107.8 %all-gather.16.cloned.1.call-start = ((), (), s32[]{:S(2)}) async-start(), calls=%async_computation.6 | async-start | bytes 2621440 | tf_op jit(solution)/shard_map/all_gather | solution.py:25
  9.6 151.5 %all-gather.14.cloned.1.call-start = ((), (), s32[]{:S(2)}) async-start(), calls=%async_computation.5 | async-start | bytes 2621440 | tf_op jit(solution)/shard_map/all_gather | solution.py:25
  10.4 240.8 %all-reduce.3.cloned.1.call-start = ((), (), s32[]{:S(2)}) async-start(), calls=%async_computation.7 | async-start | bytes 4194304 | tf_op jit(solution)/shard_map/psum | solution.py:32
  98.5 16.6 %copy-start = (bf16[1,16,32,512]{3,2,1,0:T(8,128)(2,1)S(1)}, bf16[1,16,32,512]{3,2,1,0:T(8,128)(2,1)}, u32[]{:S(2)}) copy-start(bf16[1,16,32,512]{3,2,1,0:T(8,128)(2,1)} %get-tuple-element.13) | copy-start | bytes 1572868
  115.1 46.1 %copy-start.1 = (bf16[1,16,32,512]{3,2,1,0:T(8,128)(2,1)S(1)}, bf16[1,16,32,512]{3,2,1,0:T(8,128)(2,1)}, u32[]{:S(2)}) copy-start(bf16[1,16,32,512]{3,2,1,0:T(8,128)(2,1)} %get-tuple-element.14) | copy-start | bytes 1572868
  161.2 5.0 copy-start.2
  166.0 0.8 copy-start.3
  166.1 132.5 %all-gather.10.cloned.1.call-start = ((), (), s32[]{:S(2)}) async-start(), calls=%async_computation.2 | async-start | bytes 2621440 | tf_op jit(solution)/shard_map/all_gather | solution.py:45
  253.7 90.8 %all-gather.12.cloned.1.call-start = ((), (), s32[]{:S(2)}) async-start(), calls=%async_computation.3 | async-start | bytes 2621440 | tf_op jit(solution)/shard_map/all_gather | solution.py:45
  257.0 308.6 %reduce-scatter.2.cloned.1.call-start = ((), (), s32[]{:S(2)}) async-start(), calls=%async_computation.4 | async-start | bytes 18874368 | tf_op jit(solution)/shard_map/reduce_scatter | solution.py:52
Sparse Core Ops, SparseCore 0:
  9.2 58.5 all-gather.7
  69.4 45.6 all-gather.15
  116.7 44.4 all-gather.13
  166.2 84.9 all-reduce.2
  253.9 44.6 all-gather.9
  300.0 44.4 all-gather.11
  450.7 114.8 reduce-scatter.1
where the time goes:
time: 574 us; the launch traced here: 572 us
  waiting for transfers between devices  383 us (67%)
  other arithmetic  76.9 us (13%)
  local copies, waits for them, and re-layouts  74.4 us (13%)
  matrix products  23.9 us (4%)
  between operations  13.7 us (2%)
    reduce_scatter x1, waiting for transfers between devices, body(): lax.psum_scatter(totals.reshape(nblocks, rows_mine, nbasis), 'grid', scat...  115 us
    psum x1, waiting for transfers between devices, body(): intersection = lax.psum(intersection_part, 'rows')  84.3 us
    all_gather x2, waiting for transfers between devices, body(): lax.all_gather(potential, 'rows', axis=1, tiled=True)  71.1 us
    scatter-add x2, other arithmetic, body(): totals.at[blocks[:, None], :, blocks[None, :], :]  70.6 us
    all_gather x1, waiting for transfers between devices, body(): stripe = lax.all_gather(density, 'grid', axis=2, tiled=True)  57.3 us
    all_gather x2, waiting for transfers between devices, body(): lax.all_gather(local_values, 'rows', axis=1, tiled=True)  53.9 us
    gather x2, local copies, waits for them, and re-layouts, body(): jnp.take(stripe, blocks, axis=0)  12.4 us
    reshape x1, local copies, waits for them, and re-layouts, body(): totals.reshape(nblocks, rows_mine, nbasis)  11.7 us
  transfers between devices with their start and end apart: 7, of which 7 were waited for; matrix products, arithmetic and copies ran while one was open for 11% of the time, Pallas kernels for 0%

commit v1 on v0

--- a/solution.py
+++ b/solution.py
@@ -19,11 +19,27 @@
         chosen = jnp.take(row_pick, blocks, axis=1)
         local_values = basis_values[batch_index]
         x_mine = local_values.reshape(nsig * rows_mine, npoints)
-        fsum = jnp.einsum(
-            "mtk,tkp->mp",
-            chosen,
-            lax.all_gather(local_values, "rows", axis=1, tiled=True),
-            preferred_element_type=jnp.float32,
+
+        def wall_draft(obj, dim_no, point):
+            part_now, aux = (lax.axis_size("rows"), lax.axis_index("rows"))
+            in_order = [(it, (it - 1) % part_now) for it in range(part_now)]
+            met_up = obj.shape[dim_no]
+            m_next = obj
+            val = point(m_next, aux * met_up)
+            for i0 in range(1, part_now):
+                m_next = lax.ppermute(m_next, axis_name="rows", perm=in_order)
+                val = val + point(m_next, (aux + i0) % part_now * met_up)
+            return val
+
+        fsum = wall_draft(
+            local_values,
+            1,
+            lambda shard, offset: jnp.einsum(
+                "mtk,tkp->mp",
+                lax.dynamic_slice_in_dim(chosen, offset, shard.shape[1], axis=2),
+                shard,
+                preferred_element_type=jnp.float32,
+            ),
         )
         fmat = fsum.astype(jnp.bfloat16)
         intersection_part = lax.dot_general(

time: 574 us -> 536 us (0.934)
  waiting for transfers between devices: 383 us -> 308 us
  starting transfers between devices: 0.43 us -> 23.3 us
    all_gather x2 -> x0, waiting for transfers between devices: 53.9 us -> none  [body(): lax.all_gather(local_values, 'rows', axis=1, tiled=True)]
    all_gather x1, waiting for transfers between devices: 57.3 us -> 3.5 us  [body(): stripe = lax.all_gather(density, 'grid', axis=2, tiled=True)]
    ppermute x0 -> x6, waiting for transfers between devices: none -> 32.6 us  [wall_draft(): m_next = lax.ppermute(m_next, axis_name='rows', perm=in_order)]
    ppermute x0 -> x6, starting transfers between devices: none -> 22.9 us  [wall_draft(): m_next = lax.ppermute(m_next, axis_name='rows', perm=in_order)]
    dot_general x0 -> x6, matrix products: none -> 6.85 us  [body(): jnp.einsum('mtk,tkp->mp', lax.dynamic_slice_in_dim(chosen, offset, shard....]
  transfers between devices with their start and end apart: 7 -> 11, of which waited for: 7 -> 9; matrix products, arithmetic and copies ran while one was open for 11% -> 14% of each run, Pallas kernels for 0% -> 0%
where the time goes in v1:
time: 536 us; the launch traced here: 535 us
  waiting for transfers between devices  308 us (57%)
  other arithmetic  82.1 us (15%)
  local copies, waits for them, and re-layouts  79.3 us (15%)
  matrix products  28.2 us (5%)
  starting transfers between devices  23.3 us (4%)
  between operations  13.4 us (2%)
    reduce_scatter x1, waiting for transfers between devices, body(): lax.psum_scatter(totals.reshape(nblocks, rows_mine, nbasis), 'grid', scat...  115 us
    psum x1, waiting for transfers between devices, body(): intersection = lax.psum(intersection_part, 'rows')  85.3 us
    all_gather x2, waiting for transfers between devices, body(): lax.all_gather(potential, 'rows', axis=1, tiled=True)  71.3 us
    scatter-add x2, other arithmetic, body(): totals.at[blocks[:, None], :, blocks[None, :], :]  70.7 us
    ppermute x6, waiting for transfers between devices, wall_draft(): m_next = lax.ppermute(m_next, axis_name='rows', perm=in_order)  32.6 us
    ppermute x6, starting transfers between devices, wall_draft(): m_next = lax.ppermute(m_next, axis_name='rows', perm=in_order)  22.9 us
    gather x2, local copies, waits for them, and re-layouts, body(): jnp.take(stripe, blocks, axis=0)  12.3 us
    reshape x1, local copies, waits for them, and re-layouts, body(): totals.reshape(nblocks, rows_mine, nbasis)  11.7 us
  transfers between devices with their start and end apart: 11, of which 9 were waited for; matrix products, arithmetic and copies ran while one was open for 14% of the time, Pallas kernels for 0%

profile of v1, /device:TPU:0, one launch (start us, length us, event | category | flops | bytes accessed | tf_op | source)
XLA Modules:
  0.0 534.5 jit_solution(6353247759422143915)
XLA Ops:
  8.8 5.1 collective-permute-start.3
  14.4 11.9 %collective-permute-done.3 = bf16[16,32,512]{2,1,0:T(8,128)(2,1)S(1)} collective-permute-done((bf16[16,32,512]{2,1,0:T(8,128)(2,1)S(1)}, bf16[16,32,512]{2,1,0:T(8,128)(2,1)S(1)}, u32[]{:S(2)}, u32[]{:S(2)}) %collective-permute-start.3) | collective-permute-done | bytes 524320 | tf_op jit(solution)/shard_map/ppermute | solution.py:30
  26.2 4.3 collective-permute-start.4
  30.5 7.0 %collective-permute-done = bf16[16,32,512]{2,1,0:T(8,128)(2,1)S(1)} collective-permute-done((bf16[16,32,512]{2,1,0:T(8,128)(2,1)S(1)}, bf16[16,32,512]{2,1,0:T(8,128)(2,1)S(1)}, u32[]{:S(2)}, u32[]{:S(2)}) %collective-permute-start) | collective-permute-done | bytes 524320 | tf_op jit(solution)/shard_map/ppermute | solution.py:30
  37.5 4.3 collective-permute-start.1
  41.8 6.9 %collective-permute-done.4 = bf16[16,32,512]{2,1,0:T(8,128)(2,1)} collective-permute-done((bf16[16,32,512]{2,1,0:T(8,128)(2,1)S(1)}, bf16[16,32,512]{2,1,0:T(8,128)(2,1)}, u32[]{:S(2)}, u32[]{:S(2)}) %collective-permute-start.4) | collective-permute-done | bytes 524320 | tf_op jit(solution)/shard_map/ppermute | solution.py:30
  48.7 4.4 collective-permute-start.5
  53.1 6.9 %collective-permute-done.1 = bf16[16,32,512]{2,1,0:T(8,128)(2,1)} collective-permute-done((bf16[16,32,512]{2,1,0:T(8,128)(2,1)S(1)}, bf16[16,32,512]{2,1,0:T(8,128)(2,1)}, u32[]{:S(2)}, u32[]{:S(2)}) %collective-permute-start.1) | collective-permute-done | bytes 524320 | tf_op jit(solution)/shard_map/ppermute | solution.py:30
  60.0 4.4 collective-permute-start.2
  64.3 3.5 all-gather.4.cloned.1.call-done
  67.8 6.2 %gather_fusion.2 = bf16[16,32,4096]{2,1,0:T(8,128)(2,1)} fusion(bf16[32,32,4096]{2,1,0:T(8,128)(2,1)} %all-gather.4.cloned.1.call-done, s32[1024]{0:T(1024)S(1)} %get-tuple-element.31), kind=kCustom, calls=%fused_computation.2.clone | custom fusion | bytes 8388672 | tf_op jit(solution)/shard_map/jit(_take)/gather | solution.py:18
  77.9 3.6 copy.26
  81.5 3.1 gather_fusion.3
  87.3 3.2 select_bitcast_fusion
  90.5 6.2 %gather_fusion = bf16[16,32,4096]{2,1,0:T(8,128)(2,1)} fusion(bf16[32,32,4096]{2,1,0:T(8,128)(2,1)} %all-gather.4.cloned.1.call-done, s32[1024]{0:T(1024)S(1)} %get-tuple-element.32), kind=kCustom, calls=%fused_computation.clone | custom fusion | bytes 8388672 | tf_op jit(solution)/shard_map/jit(_take)/gather | solution.py:18
  100.6 3.6 copy.21
  120.6 3.2 convolution_bitcast_fusion.2
  123.9 3.4 convolution_bitcast_fusion.7
  128.3 85.3 %all-reduce.3.cloned.1.call-done = (f32[512,512]{0,1:T(8,128)}, f32[512,512]{0,1:T(8,128)}) async-done(((f32[512,512]{0,1:T(8,128)}, f32[512,512]{0,1:T(8,128)}), (f32[512,512]{0,1:T(8,128)}, f32[512,512]{0,1:T(8,128)})) %all-reduce.3.cloned.1.call-update) | async-done | bytes 2097168 | tf_op jit(solution)/shard_map/psum | solution.py:48
  219.9 41.1 %all-gather.6.cloned.1.call-done = bf16[16,128,512]{2,1,0:T(8,128)(2,1)} async-done(((bf16[16,32,512]{2,1,0:T(8,128)(2,1)}), bf16[16,128,512]{2,1,0:T(8,128)(2,1)}) %all-gather.6.cloned.1.call-update) | async-done | bytes 2097168 | tf_op jit(solution)/shard_map/all_gather | solution.py:61
  261.0 4.8 convolution_bitcast_fusion.1
  265.8 5.6 %copy.23 = f32[512,16,128]{2,1,0:T(8,128)} copy(f32[512,16,128]{0,2,1:T(8,128)} %convolution_bitcast_fusion.1) | data formatting | bytes 8388608 | tf_op jit(solution)/shard_map/mp,tkp->mtk/dot_general | solution.py:58
  271.4 5.4 %copy.24 = f32[16,16,32,128]{3,2,1,0:T(8,128)} copy(f32[16,16,32,128]{3,1,2,0:T(8,128)} %bitcast.135) | data formatting | bytes 8388608 | tf_op jit(solution)/shard_map/transpose | solution.py:66
  276.8 30.1 %all-gather.8.cloned.1.call-done = bf16[16,128,512]{2,1,0:T(8,128)(2,1)} async-done(((bf16[16,32,512]{2,1,0:T(8,128)(2,1)}), bf16[16,128,512]{2,1,0:T(8,128)(2,1)}) %all-gather.8.cloned.1.call-update) | async-done | bytes 2097168 | tf_op jit(solution)/shard_map/all_gather | solution.py:61
  306.9 4.8 convolution_bitcast_fusion
  311.7 5.5 %copy.28 = f32[512,16,128]{2,1,0:T(8,128)} copy(f32[512,16,128]{0,2,1:T(8,128)} %convolution_bitcast_fusion) | data formatting | bytes 8388608 | tf_op jit(solution)/shard_map/mp,tkp->mtk/dot_general | solution.py:58
  317.3 5.5 %copy.29 = f32[16,16,32,128]{3,2,1,0:T(8,128)} copy(f32[16,16,32,128]{3,1,2,0:T(8,128)} %bitcast.136) | data formatting | bytes 8388608 | tf_op jit(solution)/shard_map/transpose | solution.py:66
  322.8 7.9 %broadcast_in_dim.45 = f32[32,32,32,128]{3,1,2,0:T(8,128)} broadcast(f32[]{:T(128)} %constant.42.clone.1), dimensions={} | broadcast | bytes 16777220 | tf_op jit(solution)/shard_map/broadcast_in_dim | solution.py:15
  330.6 35.3 %scatter_fusion = f32[32,32,32,128]{3,1,2,0:T(8,128)} fusion(f32[32,32,32,128]{3,1,2,0:T(8,128)} %broadcast_in_dim.45, s32[256]{0:T(256)S(1)} %reshape.132, f32[256,32,128]{2,1,0:T(8,128)} %bitcast.129), kind=kCustom, calls=%fused_computation.4 | custom fusion | flops 1048576 | bytes 12584960 | tf_op jit(solution)/shard_map/scatter-add | solution.py:65
  365.9 35.4 %scatter_fusion.1 = f32[32,32,32,128]{3,1,2,0:T(8,128)} fusion(f32[32,32,32,128]{3,1,2,0:T(8,128)} %scatter_fusion, s32[256]{0:T(256)S(1)} %reshape.138, f32[256,32,128]{2,1,0:T(8,128)} %bitcast.130), kind=kCustom, calls=%fused_computation.5 | custom fusion | flops 1048576 | bytes 12584960 | tf_op jit(solution)/shard_map/scatter-add | solution.py:65
  401.4 11.7 %copy_bitcast_fusion = f32[32,32,4096]{2,1,0:T(8,128)} fusion(f32[32,32,32,128]{3,1,2,0:T(8,128)} %scatter_fusion.1), kind=kLoop, calls=%fused_computation.6 | loop fusion | bytes 33554432 | tf_op jit(solution)/shard_map/reshape | solution.py:69
  413.1 114.9 %reduce-scatter.2.cloned.1.call-done = f32[32,32,512]{2,1,0:T(8,128)} async-done(((f32[32,32,4096]{2,1,0:T(8,128)}), f32[32,32,512]{2,1,0:T(8,128)}) %reduce-scatter.2.cloned.1.call-update) | async-done | bytes 2097168 | tf_op jit(solution)/shard_map/reduce_scatter | solution.py:68
  (67 shorter events, 36.8 us)
Async XLA Ops:
  6.5 35.2 %copy-start.5 = (s32[2,16]{1,0:T(2,128)S(1)}, s32[2,16]{1,0:T(2,128)}, u32[]{:S(2)}) copy-start(s32[2,16]{1,0:T(2,128)} %param.13) | copy-start | bytes 388
  6.5 61.3 %all-gather.4.cloned.1.call-start = ((), (), s32[]{:S(2)}) async-start(), calls=%async_computation.1 | async-start | bytes 9437184 | tf_op jit(solution)/shard_map/all_gather | solution.py:14
  7.3 206.4 %all-reduce.3.cloned.1.call-start = ((), (), s32[]{:S(2)}) async-start(), calls=%async_computation.5 | async-start | bytes 4194304 | tf_op jit(solution)/shard_map/psum | solution.py:48
  8.8 17.4 %collective-permute-start.3 = (bf16[16,32,512]{2,1,0:T(8,128)(2,1)S(1)}, bf16[16,32,512]{2,1,0:T(8,128)(2,1)S(1)}, u32[]{:S(2)}, u32[]{:S(2)}) collective-permute-start(bf16[16,32,512]{2,1,0:T(8,128)(2,1)S(1)} %get-tuple-element.13), channel_id=1, source_target_pairs={{0,3},{1,0},{2,1},{3,2},{4,7},{5,4},{6,5},{7,6},{8,11},{9,8},{10,9... | collective-permute-start | bytes 1572872 | tf_op jit(solution)/shard_map/ppermute | solution.py:30
  13.9 23.5 %collective-permute-start = (bf16[16,32,512]{2,1,0:T(8,128)(2,1)S(1)}, bf16[16,32,512]{2,1,0:T(8,128)(2,1)S(1)}, u32[]{:S(2)}, u32[]{:S(2)}) collective-permute-start(bf16[16,32,512]{2,1,0:T(8,128)(2,1)S(1)} %get-tuple-element.14), channel_id=1, source_target_pairs={{0,3},{1,0},{2,1},{3,2},{4,7},{5,4},{6,5},{7,6},{8,11},{9,8},{10,9... | collective-permute-start | bytes 1572872 | tf_op jit(solution)/shard_map/ppermute | solution.py:30
  26.2 47.8 %copy-start.6 = (bf16[16,32,512]{2,1,0:T(8,128)(2,1)}, bf16[16,32,512]{2,1,0:T(8,128)(2,1)S(1)}, u32[]{:S(2)}) copy-start(bf16[16,32,512]{2,1,0:T(8,128)(2,1)S(1)} %collective-permute-done.3) | copy-start | bytes 1572868
  26.2 22.5 %collective-permute-start.4 = (bf16[16,32,512]{2,1,0:T(8,128)(2,1)S(1)}, bf16[16,32,512]{2,1,0:T(8,128)(2,1)}, u32[]{:S(2)}, u32[]{:S(2)}) collective-permute-start(bf16[16,32,512]{2,1,0:T(8,128)(2,1)S(1)} %collective-permute-done.3), channel_id=1, source_target_pairs={{0,3},{1,0},{2,1},{3,2},{4,7},{5,4},{6,5},{7,6},{8,11},{9,8},{10,9... | collective-permute-start | bytes 1572872 | tf_op jit(solution)/shard_map/ppermute | solution.py:30
  37.5 36.5 %copy-start.8 = (bf16[16,32,512]{2,1,0:T(8,128)(2,1)}, bf16[16,32,512]{2,1,0:T(8,128)(2,1)S(1)}, u32[]{:S(2)}) copy-start(bf16[16,32,512]{2,1,0:T(8,128)(2,1)S(1)} %collective-permute-done) | copy-start | bytes 1572868
  37.5 22.5 %collective-permute-start.1 = (bf16[16,32,512]{2,1,0:T(8,128)(2,1)S(1)}, bf16[16,32,512]{2,1,0:T(8,128)(2,1)}, u32[]{:S(2)}, u32[]{:S(2)}) collective-permute-start(bf16[16,32,512]{2,1,0:T(8,128)(2,1)S(1)} %collective-permute-done), channel_id=1, source_target_pairs={{0,3},{1,0},{2,1},{3,2},{4,7},{5,4},{6,5},{7,6},{8,11},{9,8},{10,9... | collective-permute-start | bytes 1572872 | tf_op jit(solution)/shard_map/ppermute | solution.py:30
  48.7 71.9 %collective-permute-start.5 = (bf16[16,32,512]{2,1,0:T(8,128)(2,1)}, bf16[16,32,512]{2,1,0:T(8,128)(2,1)}, u32[]{:S(2)}, u32[]{:S(2)}) collective-permute-start(bf16[16,32,512]{2,1,0:T(8,128)(2,1)} %collective-permute-done.4), channel_id=1, source_target_pairs={{0,3},{1,0},{2,1},{3,2},{4,7},{5,4},{6,5},{7,6},{8,11},{9,8},{10,9... | collective-permute-start | bytes 1572872 | tf_op jit(solution)/shard_map/ppermute | solution.py:30
  60.0 63.9 %collective-permute-start.2 = (bf16[16,32,512]{2,1,0:T(8,128)(2,1)}, bf16[16,32,512]{2,1,0:T(8,128)(2,1)}, u32[]{:S(2)}, u32[]{:S(2)}) collective-permute-start(bf16[16,32,512]{2,1,0:T(8,128)(2,1)} %collective-permute-done.1), channel_id=1, source_target_pairs={{0,3},{1,0},{2,1},{3,2},{4,7},{5,4},{6,5},{7,6},{8,11},{9,8},{10,9... | collective-permute-start | bytes 1572872 | tf_op jit(solution)/shard_map/ppermute | solution.py:30
  109.9 2.2 copy-start
  109.9 2.5 copy-start.2
  112.3 5.8 %copy-start.1 = (bf16[512,16,128]{0,2,1:T(8,128)(2,1)}, bf16[512,16,128]{0,2,1:T(8,128)(2,1)S(1)}, u32[]{:S(2)}) copy-start(bf16[512,16,128]{0,2,1:T(8,128)(2,1)S(1)} %select_bitcast_fusion.1) | copy-start | bytes 6291460
  112.8 1.3 copy-start.7
  114.1 1.0 copy-start.9
  123.9 3.7 copy-start.3
  127.3 1.0 copy-start.4
  127.3 133.7 %all-gather.6.cloned.1.call-start = ((), (), s32[]{:S(2)}) async-start(), calls=%async_computation.2 | async-start | bytes 2621440 | tf_op jit(solution)/shard_map/all_gather | solution.py:61
  216.2 90.8 %all-gather.8.cloned.1.call-start = ((), (), s32[]{:S(2)}) async-start(), calls=%async_computation.3 | async-start | bytes 2621440 | tf_op jit(solution)/shard_map/all_gather | solution.py:61
  219.5 308.5 %reduce-scatter.2.cloned.1.call-start = ((), (), s32[]{:S(2)}) async-start(), calls=%async_computation.4 | async-start | bytes 18874368 | tf_op jit(solution)/shard_map/reduce_scatter | solution.py:68
Sparse Core Ops, SparseCore 0:
  9.2 58.5 all-gather.3
  127.4 86.1 all-reduce.2
  216.3 44.6 all-gather.5
  262.4 44.4 all-gather.7
  413.2 114.7 reduce-scatter.1
